TPU v7x, 32 devices: a whole 2x2x4 slice. The times are simulated.
32 devices in a mesh: owner: 4 (over y, core), rows: 8 (over z, x).
Axes of the slice: x: 2, y: 2, z: 4, core: 2. Of those that a mesh axis runs over, the one named last changes fastest.
Arguments:
- w_down: float32 [16, 6400, 4096], P('owner', None, 'rows'), may hold values from -0.109375 to 0.109375
- avg_down: bfloat16 [16, 6400, 4096], P('owner', None, 'rows'), may hold values from -0.0390625 to 0.0390625
- router_weight: float32 [4096, 16], P('rows', 'owner'), may hold values from -0.09375 to 0.09375
- router_gain: float32 [4096], P('rows'), may hold values from 0.25 to 1.75
Outputs:
- serve_down: bfloat16 [16, 6400, 4096], P('owner', 'rows')
- scale_down: float32 [16, 6400], P('owner', 'rows')
- serve_router: bfloat16 [4096, 16], replicated
All inputs are finite; a program needn't handle non-finite values.
Results may differ from a plain program's by a relative error of at most 0.0085.
Values may be sent and summed in bfloat16 or wider, within the bound.
A program may use at most 256 MiB of HBM per device.

v0:
```python
import jax
import jax.numpy as jnp
from jax import lax
from jax.sharding import PartitionSpec as P


def local(w_down, avg_down, router_weight, router_gain):
    fresh_down = w_down + avg_down.astype(jnp.float32)
    total_down = lax.psum(
        jnp.sum(fresh_down * fresh_down, axis=2).astype(jnp.bfloat16), "rows"
    ).astype(jnp.float32)
    scale_down = jnp.sqrt(total_down)
    narrow_down = (fresh_down / jnp.expand_dims(scale_down, 2)).astype(jnp.bfloat16)
    serve_down = lax.all_to_all(narrow_down, "rows", split_axis=1, concat_axis=2, tiled=True)
    scale_down = lax.dynamic_slice_in_dim(
        scale_down, lax.axis_index("rows") * serve_down.shape[1], serve_down.shape[1], axis=1
    )
    part_router = (router_weight * router_gain[:, None]).astype(jnp.bfloat16)
    row_router = lax.all_gather(part_router, "rows", axis=0, tiled=True)
    serve_router = lax.all_gather(row_router, "owner", axis=1, tiled=True)
    return (serve_down, scale_down, serve_router)


def solution(mesh):
    return jax.shard_map(
        local,
        mesh=mesh,
        in_specs=(
            P("owner", None, "rows"),
            P("owner", None, "rows"),
            P("rows", "owner"),
            P("rows"),
        ),
        out_specs=(P("owner", "rows", None), P("owner", "rows"), P()),
        check_vma=False,
    )
```

profile of v0, /device:TPU:0, one launch (start us, length us, event | category | flops | bytes accessed | tf_op | source)
XLA Modules:
  0.0 826.9 jit_solution(7862156734528137198)
XLA Ops:
  0.6 24.2 %multiply_reduce_fusion = bf16[4,6400]{1,0:T(4,128)(2,1)S(1)} fusion(f32[4,6400,512]{2,1,0:T(8,128)} %param.4, bf16[4,6400,512]{2,1,0:T(8,128)(2,1)} %param.5), kind=kLoop, calls=%fused_computation.1 | loop fusion | flops 52403200 | bytes 78694400 | tf_op jit(solution)/shard_map/reduce_sum | solution.py:10
  24.9 0.9 copy.21
  25.8 83.5 %psum.7 = bf16[4,6400]{0,1:T(8,128)(2,1)} all-reduce(bf16[4,6400]{0,1:T(8,128)(2,1)S(1)} %copy.21), channel_id=1, replica_groups=mesh['owner'=4,'rows'=8] {'rows'}, use_global_device_ids=true, to_apply=%region_1.0 | all-reduce | flops 25600 | bytes 102400 | tf_op jit(solution)/shard_map/psum | solution.py:9
  109.3 2.3 convert_sqrt_fusion
  111.6 1.2 copy.17
  112.8 34.3 %divide_convert_fusion = bf16[4,6400,512]{2,1,0:T(8,128)(2,1)} fusion(f32[4,6400,512]{2,1,0:T(8,128)} %param.4, bf16[4,6400,512]{2,1,0:T(8,128)(2,1)} %param.5, f32[4,6400]{1,0:T(4,128)S(1)} %copy.17), kind=kLoop, calls=%fused_computation | loop fusion | flops 52428800 | bytes 104960000 | tf_op jit(solution)/shard_map/convert_element_type | solution.py:13
  147.1 33.4 %copy.18 = bf16[4,6400,512]{2,0,1:T(4,128)(2,1)} copy(bf16[4,6400,512]{2,1,0:T(8,128)(2,1)} %divide_convert_fusion) | data formatting | bytes 52428800 | tf_op jit(solution)/shard_map/convert_element_type | solution.py:13
  180.5 0.0 copy-start
  180.5 0.0 copy-start.1
  180.5 6.6 all-to-all-start
  187.2 0.8 constant_dynamic-slice_fusion
  187.9 1.8 copy.20
  189.7 0.0 copy-done
  189.7 0.0 copy-done.1
  189.7 573.7 %all_gather.6 = bf16[4096,4]{0,1:T(4,128)(2,1)S(1)} all-gather(bf16[512,4]{0,1:T(4,128)(2,1)S(1)} %multiply_convert_fusion), channel_id=1, replica_groups=mesh['owner'=4,'rows'=8] {'rows'}, dimensions={0}, use_global_device_ids=true | all-gather | bytes 36864 | tf_op jit(solution)/shard_map/all_gather | solution.py:19
  763.4 5.4 all-gather
  768.8 0.7 reshape.9
  769.5 0.0 all-to-all-done
  769.5 18.2 %copy.19 = bf16[4,800,8,512]{3,2,1,0:T(8,128)(2,1)} copy(bf16[4,800,8,512]{3,0,1,2:T(4,128)(2,1)} %bitcast.1) | data formatting | bytes 52428800 | tf_op jit(solution)/shard_map/all_to_all | solution.py:14
  787.7 39.2 %all_to_all.16 = bf16[4,800,4096]{2,1,0:T(8,128)(2,1)} reshape(bf16[4,800,8,512]{3,2,1,0:T(8,128)(2,1)} %copy.19) | data formatting | bytes 52428800 | tf_op jit(solution)/shard_map/all_to_all | solution.py:14
  (1 shorter events, 0.0 us)
Async XLA Ops:
  180.5 9.2 %copy-start = (f32[512,4]{0,1:T(4,128)S(1)}, f32[512,4]{0,1:T(4,128)}, u32[]{:S(2)}) copy-start(f32[512,4]{0,1:T(4,128)} %param.6) | copy-start | bytes 24580
  180.5 9.2 %copy-start.1 = (f32[512]{0:T(512)S(1)}, f32[512]{0:T(512)}, u32[]{:S(2)}) copy-start(f32[512]{0:T(512)} %param.7) | copy-start | bytes 6148
  180.5 589.0 %all-to-all-start = ((bf16[4,6400,512]{2,0,1:T(4,128)(2,1)}), bf16[4,6400,512]{2,0,1:T(4,128)(2,1)}, u32[]{:S(2)}, u32[]{:S(2)}) async-start(bf16[4,6400,512]{2,0,1:T(4,128)(2,1)} %copy.18), calls=%async_computation | async-start | bytes 52428800 | tf_op jit(solution)/shard_map/all_to_all | solution.py:14
where the time goes:
time: 828 us; the launch traced here: 827 us
  blocking collectives  663 us (80%)
  local copies, waits for them, and re-layouts  96.2 us (12%)
  other arithmetic  60.8 us (7%)
    all_gather x1, blocking collectives, local(): row_router = lax.all_gather(part_router, 'rows', axis=0, tiled=True)  574 us
    psum x1, blocking collectives, local(): lax.psum(jnp.sum(fresh_down * fresh_down, axis=2).astype(jnp.bfloat16), '...  83.5 us
    all_to_all x2, local copies, waits for them, and re-layouts, local(): lax.all_to_all(narrow_down, 'rows', split_axis=1, concat_axis=2, tiled=True)  57.4 us
    convert_element_type x1, other arithmetic, local(): (fresh_down / jnp.expand_dims(scale_down, 2)).astype(jnp.bfloat16)  34.3 us
    convert_element_type x1, local copies, waits for them, and re-layouts, local(): (fresh_down / jnp.expand_dims(scale_down, 2)).astype(jnp.bfloat16)  33.4 us
    reduce_sum x1, other arithmetic, local(): jnp.sum(fresh_down * fresh_down, axis=2).astype(jnp.bfloat16)  24.2 us
  transfers between devices with their start and end apart: 1, of which 0 were waited for; matrix products, arithmetic and copies ran while one was open for 0% of the time, Pallas kernels for 0%

commit v1 on v0

--- a/solution.py
+++ b/solution.py
@@ -2,6 +2,17 @@
 import jax.numpy as jnp
 from jax import lax
 from jax.sharding import PartitionSpec as P
+
+
+def split_up(x, dim, count):
+    before, after = (x.shape[:dim], x.shape[dim + 1 :])
+    return jnp.moveaxis(x.reshape(*before, count, -1, *after), dim, 0)
+
+
+def in_order(parts, dim):
+    dims = list(parts.shape[1:])
+    dims[dim] *= parts.shape[0]
+    return jnp.moveaxis(parts, 0, dim).reshape(dims)
 
 
 def local(w_down, avg_down, router_weight, router_gain):
@@ -11,7 +22,15 @@
     ).astype(jnp.float32)
     scale_down = jnp.sqrt(total_down)
     narrow_down = (fresh_down / jnp.expand_dims(scale_down, 2)).astype(jnp.bfloat16)
-    serve_down = lax.all_to_all(narrow_down, "rows", split_axis=1, concat_axis=2, tiled=True)
+    size, position = (lax.axis_size("rows"), lax.axis_index("rows"))
+    blocks = split_up(narrow_down, 1, size)
+    out = blocks
+    for lap in range(1, size):
+        target, source = ((position + lap) % size, (position - lap) % size)
+        sent = lax.dynamic_index_in_dim(blocks, target, 0)
+        partner_block = lax.ppermute(sent, "rows", [(i, (i + lap) % size) for i in range(size)])
+        out = lax.dynamic_update_slice_in_dim(out, partner_block, source, axis=0)
+    serve_down = in_order(out, 2)
     scale_down = lax.dynamic_slice_in_dim(
         scale_down, lax.axis_index("rows") * serve_down.shape[1], serve_down.shape[1], axis=1
     )

time: 828 us -> 741 us (0.89)
  blocking collectives: 663 us -> 475 us
  waiting for transfers between devices: 0.01 us -> 71.6 us
  starting transfers between devices: 6.64 us -> 74.9 us
  local copies, waits for them, and re-layouts: 96.2 us -> 59.4 us
    all_gather x1, blocking collectives: 574 us -> 430 us  [local(): row_router = lax.all_gather(part_router, 'rows', axis=0, tiled=True)]
    ppermute x0 -> x7, starting transfers between devices: none -> 74.9 us  [local(): lax.ppermute(sent, 'rows', [(i, (i + lap) % size) for i in range(size)])]
    ppermute x0 -> x7, waiting for transfers between devices: none -> 71.6 us  [local(): lax.ppermute(sent, 'rows', [(i, (i + lap) % size) for i in range(size)])]
    all_to_all x2 -> x0, local copies, waits for them, and re-layouts: 57.4 us -> none  [local(): lax.all_to_all(narrow_down, 'rows', split_axis=1, concat_axis=2, tiled=True)]
    psum x1, blocking collectives: 83.5 us -> 39.3 us  [local(): lax.psum(jnp.sum(fresh_down * fresh_down, axis=2).astype(jnp.bfloat16), '...]
    convert_element_type x1 -> x0, local copies, waits for them, and re-layouts: 33.4 us -> none  [local(): (fresh_down / jnp.expand_dims(scale_down, 2)).astype(jnp.bfloat16)]
    dynamic_update_slice x0 -> x7, local copies, waits for them, and re-layouts: none -> 25.3 us  [local(): out = lax.dynamic_update_slice_in_dim(out, partner_block, source, axis=0)]
    reshape x0 -> x1, local copies, waits for them, and re-layouts: none -> 17.9 us  [in_order(): return jnp.moveaxis(parts, 0, dim).reshape(dims)]
  transfers between devices with their start and end apart: 1 -> 7, of which waited for: 0 -> 1; matrix products, arithmetic and copies ran while one was open for 0% -> 3% of each run, Pallas kernels for 0% -> 0%
where the time goes in v1:
time: 741 us; the launch traced here: 740 us
  blocking collectives  475 us (64%)
  starting transfers between devices  74.9 us (10%)
  waiting for transfers between devices  71.6 us (10%)
  local copies, waits for them, and re-layouts  59.4 us (8%)
  other arithmetic  58.6 us (8%)
    all_gather x1, blocking collectives, local(): row_router = lax.all_gather(part_router, 'rows', axis=0, tiled=True)  430 us
    ppermute x7, starting transfers between devices, local(): lax.ppermute(sent, 'rows', [(i, (i + lap) % size) for i in range(size)])  74.9 us
    ppermute x7, waiting for transfers between devices, local(): lax.ppermute(sent, 'rows', [(i, (i + lap) % size) for i in range(size)])  71.6 us
    psum x1, blocking collectives, local(): lax.psum(jnp.sum(fresh_down * fresh_down, axis=2).astype(jnp.bfloat16), '...  39.3 us
    convert_element_type x1, other arithmetic, local(): (fresh_down / jnp.expand_dims(scale_down, 2)).astype(jnp.bfloat16)  34.3 us
    dynamic_update_slice x7, local copies, waits for them, and re-layouts, local(): out = lax.dynamic_update_slice_in_dim(out, partner_block, source, axis=0)  25.3 us
    reduce_sum x1, other arithmetic, local(): jnp.sum(fresh_down * fresh_down, axis=2).astype(jnp.bfloat16)  24.2 us
    reshape x1, local copies, waits for them, and re-layouts, in_order(): return jnp.moveaxis(parts, 0, dim).reshape(dims)  17.9 us
  transfers between devices with their start and end apart: 7, of which 1 were waited for; matrix products, arithmetic and copies ran while one was open for 3% of the time, Pallas kernels for 0%

profile of v1, /device:TPU:0, one launch (start us, length us, event | category | flops | bytes accessed | tf_op | source)
XLA Modules:
  0.0 740.2 jit_solution(11643379839295329696)
XLA Ops:
  0.7 24.2 %multiply_reduce_fusion = bf16[4,6400]{1,0:T(4,128)(2,1)S(1)} fusion(f32[4,6400,512]{2,1,0:T(8,128)} %param.4, bf16[4,6400,512]{2,1,0:T(8,128)(2,1)} %param.5), kind=kLoop, calls=%fused_computation.1 | loop fusion | flops 52403200 | bytes 78694400 | tf_op jit(solution)/shard_map/reduce_sum | solution.py:21
  25.0 39.3 %psum.7 = bf16[4,6400]{1,0:T(4,128)(2,1)S(1)} all-reduce(bf16[4,6400]{1,0:T(4,128)(2,1)S(1)} %multiply_reduce_fusion), channel_id=1, replica_groups=mesh['owner'=4,'rows'=8] {'rows'}, use_global_device_ids=true, to_apply=%region_1.0 | all-reduce | flops 25600 | bytes 102400 | tf_op jit(solution)/shard_map/psum | solution.py:20
  64.3 0.1 convert_sqrt_fusion
  64.4 34.3 %divide_convert_fusion = bf16[4,6400,512]{2,1,0:T(8,128)(2,1)} fusion(f32[4,6400,512]{2,1,0:T(8,128)} %param.4, bf16[4,6400,512]{2,1,0:T(8,128)(2,1)} %param.5, f32[4,6400]{1,0:T(4,128)S(1)} %convert_sqrt_fusion), kind=kLoop, calls=%fused_computation | loop fusion | flops 52428800 | bytes 104960000 | tf_op jit(solution)/shard_map/convert_element_type | solution.py:24
  98.7 0.0 copy-start
  98.7 0.0 copy-start.1
  98.7 14.9 %dynamic-slice_bitcast_fusion = (bf16[1,4,800,512]{3,2,0,1:T(8,128)(2,1)}, bf16[1,4,800,512]{3,2,0,1:T(8,128)(2,1)}, bf16[1,4,800,512]{3,2,0,1:T(8,128)(2,1)}, b...) fusion(bf16[4,8,800,512]{3,2,1,0:T(8,128)(2,1)} %bitcast.38, ...), kind=kLoop, calls=%fused_computation.3 | loop fusion | bytes 45875228 | tf_op jit(solution)/shard_map/jit(dynamic_index_in_dim)/dynamic_slice | solution.py:30
  113.6 0.1 collective-permute-start
  113.7 0.1 collective-permute-start.1
  113.8 2.5 collective-permute-start.2
  116.2 2.7 collective-permute-start.3
  119.0 0.0 collective-permute-start.4
  119.0 71.6 %collective-permute-done = bf16[1,4,800,512]{3,2,0,1:T(8,128)(2,1)} collective-permute-done((bf16[1,4,800,512]{3,2,0,1:T(8,128)(2,1)}, bf16[1,4,800,512]{3,2,0,1:T(8,128)(2,1)}, u32[]{:S(2)}, u32[]{:S(2)}) %collective-permute-start) | collective-permute-done | bytes 3276832 | tf_op jit(solution)/shard_map/ppermute | solution.py:31
  190.6 0.0 collective-permute-start.5
  190.6 0.0 collective-permute-done.1
  190.6 69.5 %collective-permute-start.6 = (bf16[1,4,800,512]{3,2,0,1:T(8,128)(2,1)}, bf16[1,4,800,512]{3,2,0,1:T(8,128)(2,1)}, u32[]{:S(2)}, u32[]{:S(2)}) collective-permute-start(bf16[1,4,800,512]{3,2,0,1:T(8,128)(2,1)} %get-tuple-element.3), channel_id=1, source_target_pairs={{0,7},{1,0},{2,1},{3,2},{4,3},{5,4},{6,5},{7,6},{8,15},{9,8},{10,9... | collective-permute-start | bytes 9830408 | tf_op jit(solution)/shard_map/ppermute | solution.py:31
  260.1 0.0 copy-done
  260.1 0.0 copy-done.1
  260.1 430.1 %all_gather.6 = bf16[4096,4]{0,1:T(4,128)(2,1)S(1)} all-gather(bf16[512,4]{0,1:T(4,128)(2,1)S(1)} %multiply_convert_fusion), channel_id=1, replica_groups=mesh['owner'=4,'rows'=8] {'rows'}, dimensions={0}, use_global_device_ids=true | all-gather | bytes 36864 | tf_op jit(solution)/shard_map/all_gather | solution.py:38
  690.2 5.4 all-gather
  695.6 0.7 reshape.24
  696.3 0.7 constant_dynamic-slice_fusion
  697.0 3.9 constant_dynamic-update-slice_fusion.6
  700.9 4.0 constant_dynamic-update-slice_fusion.5
  704.8 0.0 collective-permute-done.2
  704.8 3.9 constant_dynamic-update-slice_fusion.4
  708.7 0.0 collective-permute-done.3
  708.7 3.8 constant_dynamic-update-slice_fusion.3
  712.5 0.0 collective-permute-done.4
  712.5 2.0 constant_dynamic-update-slice_fusion.2
  714.6 0.0 collective-permute-done.5
  714.6 3.9 constant_dynamic-update-slice_fusion.1
  718.4 0.0 collective-permute-done.6
  718.4 3.9 constant_dynamic-update-slice_fusion
  722.3 17.9 %copy.24 = bf16[4,8,100,8,512]{4,3,1,2,0:T(8,128)(2,1)} copy(bf16[4,8,100,8,512]{4,3,2,1,0:T(8,128)(2,1)} %bitcast.40) | data formatting | bytes 52428800 | tf_op jit(solution)/shard_map/reshape | solution.py:15
  (1 shorter events, 0.0 us)
Async XLA Ops:
  98.7 161.5 %copy-start = (f32[512,4]{0,1:T(4,128)S(1)}, f32[512,4]{0,1:T(4,128)}, u32[]{:S(2)}) copy-start(f32[512,4]{0,1:T(4,128)} %param.6) | copy-start | bytes 24580
  98.7 161.5 %copy-start.1 = (f32[512]{0:T(512)S(1)}, f32[512]{0:T(512)}, u32[]{:S(2)}) copy-start(f32[512]{0:T(512)} %param.7) | copy-start | bytes 6148
  113.6 77.0 %collective-permute-start = (bf16[1,4,800,512]{3,2,0,1:T(8,128)(2,1)}, bf16[1,4,800,512]{3,2,0,1:T(8,128)(2,1)}, u32[]{:S(2)}, u32[]{:S(2)}) collective-permute-start(bf16[1,4,800,512]{3,2,0,1:T(8,128)(2,1)} %get-tuple-element.9), channel_id=1, source_target_pairs={{0,1},{1,2},{2,3},{3,4},{4,5},{5,6},{6,7},{7,0},{8,9},{9,10},{10,1... | collective-permute-start | bytes 9830408 | tf_op jit(solution)/shard_map/ppermute | solution.py:31
  113.7 76.9 %collective-permute-start.1 = (bf16[1,4,800,512]{3,2,0,1:T(8,128)(2,1)S(1)}, bf16[1,4,800,512]{3,2,0,1:T(8,128)(2,1)}, u32[]{:S(2)}, u32[]{:S(2)}) collective-permute-start(bf16[1,4,800,512]{3,2,0,1:T(8,128)(2,1)S(1)} %get-tuple-element.8), channel_id=1, source_target_pairs={{0,2},{1,3},{2,4},{3,5},{4,6},{5,7},{6,0},{7,1},{8,10},{9,11},{10,... | collective-permute-start | bytes 9830408 | tf_op jit(solution)/shard_map/ppermute | solution.py:31
  113.8 591.1 %collective-permute-start.2 = (bf16[1,4,800,512]{3,2,0,1:T(8,128)(2,1)}, bf16[1,4,800,512]{3,2,0,1:T(8,128)(2,1)}, u32[]{:S(2)}, u32[]{:S(2)}) collective-permute-start(bf16[1,4,800,512]{3,2,0,1:T(8,128)(2,1)} %get-tuple-element.7), channel_id=1, source_target_pairs={{0,3},{1,4},{2,5},{3,6},{4,7},{5,0},{6,1},{7,2},{8,11},{9,12},{10,... | collective-permute-start | bytes 9830408 | tf_op jit(solution)/shard_map/ppermute | solution.py:31
  116.2 592.5 %collective-permute-start.3 = (bf16[1,4,800,512]{3,2,0,1:T(8,128)(2,1)}, bf16[1,4,800,512]{3,2,0,1:T(8,128)(2,1)}, u32[]{:S(2)}, u32[]{:S(2)}) collective-permute-start(bf16[1,4,800,512]{3,2,0,1:T(8,128)(2,1)} %get-tuple-element.6), channel_id=1, source_target_pairs={{0,4},{1,5},{2,6},{3,7},{4,0},{5,1},{6,2},{7,3},{8,12},{9,13},{10,... | collective-permute-start | bytes 9830408 | tf_op jit(solution)/shard_map/ppermute | solution.py:31
  119.0 593.6 %collective-permute-start.4 = (bf16[1,4,800,512]{3,2,0,1:T(8,128)(2,1)}, bf16[1,4,800,512]{3,2,0,1:T(8,128)(2,1)S(1)}, u32[]{:S(2)}, u32[]{:S(2)}) collective-permute-start(bf16[1,4,800,512]{3,2,0,1:T(8,128)(2,1)} %get-tuple-element.5), channel_id=1, source_target_pairs={{0,5},{1,6},{2,7},{3,0},{4,1},{5,2},{6,3},{7,4},{8,13},{9,14},{10,... | collective-permute-start | bytes 9830408 | tf_op jit(solution)/shard_map/ppermute | solution.py:31
  190.6 524.0 %collective-permute-start.5 = (bf16[1,4,800,512]{3,2,0,1:T(8,128)(2,1)}, bf16[1,4,800,512]{3,2,0,1:T(8,128)(2,1)}, u32[]{:S(2)}, u32[]{:S(2)}) collective-permute-start(bf16[1,4,800,512]{3,2,0,1:T(8,128)(2,1)} %get-tuple-element.4), channel_id=1, source_target_pairs={{0,6},{1,7},{2,0},{3,1},{4,2},{5,3},{6,4},{7,5},{8,14},{9,15},{10,... | collective-permute-start | bytes 9830408 | tf_op jit(solution)/shard_map/ppermute | solution.py:31
  190.6 527.9 %collective-permute-start.6 = (bf16[1,4,800,512]{3,2,0,1:T(8,128)(2,1)}, bf16[1,4,800,512]{3,2,0,1:T(8,128)(2,1)}, u32[]{:S(2)}, u32[]{:S(2)}) collective-permute-start(bf16[1,4,800,512]{3,2,0,1:T(8,128)(2,1)} %get-tuple-element.3), channel_id=1, source_target_pairs={{0,7},{1,0},{2,1},{3,2},{4,3},{5,4},{6,5},{7,6},{8,15},{9,8},{10,9... | collective-permute-start | bytes 9830408 | tf_op jit(solution)/shard_map/ppermute | solution.py:31

commit v2 on v0

--- a/solution.py
+++ b/solution.py
@@ -6,8 +6,9 @@
 
 def local(w_down, avg_down, router_weight, router_gain):
     fresh_down = w_down + avg_down.astype(jnp.float32)
-    total_down = lax.psum(
-        jnp.sum(fresh_down * fresh_down, axis=2).astype(jnp.bfloat16), "rows"
+    total_down = jnp.sum(
+        lax.all_gather(jnp.sum(fresh_down * fresh_down, axis=2).astype(jnp.bfloat16), "rows"),
+        axis=0,
     ).astype(jnp.float32)
     scale_down = jnp.sqrt(total_down)
     narrow_down = (fresh_down / jnp.expand_dims(scale_down, 2)).astype(jnp.bfloat16)

time: 828 us -> 779 us (0.941)
  blocking collectives: 663 us -> 618 us
    psum x1 -> x0, blocking collectives: 83.5 us -> none  [local(): lax.psum(jnp.sum(fresh_down * fresh_down, axis=2).astype(jnp.bfloat16), '...]
    all_gather x0 -> x1, blocking collectives: none -> 32.8 us  [local(): lax.all_gather(jnp.sum(fresh_down * fresh_down, axis=2).astype(jnp.bfloat...]
where the time goes in v2:
time: 779 us; the launch traced here: 777 us
  blocking collectives  618 us (79%)
  local copies, waits for them, and re-layouts  93.8 us (12%)
  other arithmetic  58.8 us (8%)
    all_gather x1, blocking collectives, local(): row_router = lax.all_gather(part_router, 'rows', axis=0, tiled=True)  579 us
    all_to_all x2, local copies, waits for them, and re-layouts, local(): lax.all_to_all(narrow_down, 'rows', split_axis=1, concat_axis=2, tiled=True)  57.4 us
    convert_element_type x1, other arithmetic, local(): (fresh_down / jnp.expand_dims(scale_down, 2)).astype(jnp.bfloat16)  34.3 us
    convert_element_type x1, local copies, waits for them, and re-layouts, local(): (fresh_down / jnp.expand_dims(scale_down, 2)).astype(jnp.bfloat16)  33.4 us
    all_gather x1, blocking collectives, local(): lax.all_gather(jnp.sum(fresh_down * fresh_down, axis=2).astype(jnp.bfloat...  32.8 us
    reduce_sum x1, other arithmetic, local(): jnp.sum(fresh_down * fresh_down, axis=2).astype(jnp.bfloat16)  24.2 us
  transfers between devices with their start and end apart: 1, of which 0 were waited for; matrix products, arithmetic and copies ran while one was open for 0% of the time, Pallas kernels for 0%

profile of v2, /device:TPU:0, one launch (start us, length us, event | category | flops | bytes accessed | tf_op | source)
XLA Modules:
  0.0 777.5 jit_solution(17265991484088323087)
XLA Ops:
  0.6 24.2 %multiply_reduce_fusion = bf16[4,6400]{1,0:T(4,128)(2,1)S(1)} fusion(f32[4,6400,512]{2,1,0:T(8,128)} %param.4, bf16[4,6400,512]{2,1,0:T(8,128)(2,1)} %param.5), kind=kLoop, calls=%fused_computation.1 | loop fusion | flops 52403200 | bytes 78694400 | tf_op jit(solution)/shard_map/reduce_sum | solution.py:10
  24.9 0.9 copy.21
  25.8 0.8 copy.18
  26.6 32.8 %all-gather.1 = bf16[8,4,6400]{2,1,0:T(4,128)(2,1)S(1)} all-gather(bf16[1,4,6400]{2,1,0:T(4,128)(2,1)S(1)} %copy.18), channel_id=2, replica_groups=mesh['owner'=4,'rows'=8] {'rows'}, dimensions={0}, use_global_device_ids=true | all-gather | bytes 460800 | tf_op jit(solution)/shard_map/all_gather | solution.py:10
  59.4 0.2 reduce_sum.22
  59.6 0.1 convert_sqrt_fusion
  59.6 34.3 %divide_convert_fusion = bf16[4,6400,512]{2,1,0:T(8,128)(2,1)} fusion(f32[4,6400,512]{2,1,0:T(8,128)} %param.4, bf16[4,6400,512]{2,1,0:T(8,128)(2,1)} %param.5, f32[4,6400]{1,0:T(4,128)S(1)} %convert_sqrt_fusion), kind=kLoop, calls=%fused_computation | loop fusion | flops 52428800 | bytes 104960000 | tf_op jit(solution)/shard_map/convert_element_type | solution.py:14
  93.9 0.0 copy-start
  93.9 0.0 copy-start.1
  93.9 33.4 %copy.19 = bf16[4,6400,512]{2,0,1:T(4,128)(2,1)} copy(bf16[4,6400,512]{2,1,0:T(8,128)(2,1)} %divide_convert_fusion) | data formatting | bytes 52428800 | tf_op jit(solution)/shard_map/convert_element_type | solution.py:14
  127.3 6.5 all-to-all-start
  133.8 0.0 copy-done
  133.8 0.0 copy-done.1
  133.9 579.4 %all_gather.11 = bf16[4096,4]{0,1:T(4,128)(2,1)S(1)} all-gather(bf16[512,4]{0,1:T(4,128)(2,1)S(1)} %multiply_convert_fusion), channel_id=1, replica_groups=mesh['owner'=4,'rows'=8] {'rows'}, dimensions={0}, use_global_device_ids=true | all-gather | bytes 36864 | tf_op jit(solution)/shard_map/all_gather | solution.py:20
  713.3 5.4 all-gather.2
  718.7 0.7 reshape.23
  719.4 0.7 constant_dynamic-slice_fusion
  720.1 0.0 all-to-all-done
  720.1 18.2 %copy.20 = bf16[4,800,8,512]{3,2,1,0:T(8,128)(2,1)} copy(bf16[4,800,8,512]{3,0,1,2:T(4,128)(2,1)} %bitcast.2) | data formatting | bytes 52428800 | tf_op jit(solution)/shard_map/all_to_all | solution.py:15
  738.3 39.2 %all_to_all.16 = bf16[4,800,4096]{2,1,0:T(8,128)(2,1)} reshape(bf16[4,800,8,512]{3,2,1,0:T(8,128)(2,1)} %copy.20) | data formatting | bytes 52428800 | tf_op jit(solution)/shard_map/all_to_all | solution.py:15
  (1 shorter events, 0.0 us)
Async XLA Ops:
  93.9 39.9 %copy-start = (f32[512,4]{0,1:T(4,128)S(1)}, f32[512,4]{0,1:T(4,128)}, u32[]{:S(2)}) copy-start(f32[512,4]{0,1:T(4,128)} %param.6) | copy-start | bytes 24580
  93.9 39.9 %copy-start.1 = (f32[512]{0:T(512)S(1)}, f32[512]{0:T(512)}, u32[]{:S(2)}) copy-start(f32[512]{0:T(512)} %param.7) | copy-start | bytes 6148
  127.3 592.7 %all-to-all-start = ((bf16[4,6400,512]{2,0,1:T(4,128)(2,1)}), bf16[4,6400,512]{2,0,1:T(4,128)(2,1)}, u32[]{:S(2)}, u32[]{:S(2)}) async-start(bf16[4,6400,512]{2,0,1:T(4,128)(2,1)} %copy.19), calls=%async_computation | async-start | bytes 52428800 | tf_op jit(solution)/shard_map/all_to_all | solution.py:15
